TPU v7x, 32 devices: a whole 2x2x4 slice. The times are simulated.
32 devices in a mesh: row: 8 (over z, core), col: 4 (over y, x).
Axes of the slice: x: 2, y: 2, z: 4, core: 2. Of those that a mesh axis runs over, the one named last changes fastest.
Arguments:
- tokens: bfloat16 [12288, 2048], P('row', 'col'), may hold values from -6 to 6
- weight_query: bfloat16 [2048, 2048], P('row', 'col'), may hold values from -0.125 to 0.125
- weight_key: bfloat16 [2048, 2048], P('row', 'col'), may hold values from -0.125 to 0.125
- weight_value: bfloat16 [2048, 2048], P('row', 'col'), may hold values from -0.125 to 0.125
- weight_output: bfloat16 [2048, 2048], P('col', 'row'), may hold values from -0.125 to 0.125
- weight_gate: bfloat16 [2048, 8192], P('row', 'col'), may hold values from -0.125 to 0.125
- weight_up: bfloat16 [2048, 8192], P('row', 'col'), may hold values from -0.125 to 0.125
- weight_down: bfloat16 [8192, 2048], P('col', 'row'), may hold values from -0.0625 to 0.0625
- gain_query: float32 [2048], P('col'), may hold values from 0.25 to 1.75
- gain_key: float32 [2048], P('col'), may hold values from 0.25 to 1.75
- gain_attention: float32 [2048], replicated, may hold values from 0.5 to 1.5
- gain_feedforward: float32 [2048], replicated, may hold values from 0.5 to 1.5
- positions: int32 [12288], P('row'), may hold values from 0 to 1279, as said below
- segments: int32 [12288], P('row'), may hold values from 0 to 2, as said below
- cotangent: bfloat16 [12288, 2048], P('row', 'col'), may hold values from -6 to 6
Outputs:
- activations: bfloat16 [12288, 2048], P('row', 'col')
- input_grad: float32 [12288, 2048], P('row', 'col')
- query_weight_grad: float32 [2048, 2048], P('row', 'col')
- key_weight_grad: float32 [2048, 2048], P('row', 'col')
- value_weight_grad: float32 [2048, 2048], P('row', 'col')
- output_weight_grad: float32 [2048, 2048], P('col', 'row')
- gate_weight_grad: float32 [2048, 8192], P('row', 'col')
- up_weight_grad: float32 [2048, 8192], P('row', 'col')
- down_weight_grad: float32 [8192, 2048], P('col', 'row')
- query_gain_grad: float32 [2048], P('col')
- key_gain_grad: float32 [2048], P('col')
- attention_gain_grad: float32 [2048], replicated
- feedforward_gain_grad: float32 [2048], replicated
Inputs may be any that keep to these rules, and one draw needn't show every extreme that they name: The 1536 rows of each index of row form one group: the prompt's 1024 rows are consecutive with segment 0 and positions 0 to 1023; each continuation has 256 consecutive rows, one segment of 1 to 2 (each once a group) and positions 1024 to 1279 in order; the prompt lies before, between or after whole continuations. `segments`: segment ids of the layout described for positions.
All inputs are finite; a program needn't handle non-finite values.
Results may differ from a plain program's by a relative error of at most 0.02.
Values may be sent and summed in bfloat16 or wider, within the bound.
A program may use at most 320 MiB of HBM per device.

v0:
```python
import jax
import jax.numpy as jnp
from jax import lax
from jax.sharding import PartitionSpec as P

D = 2048
HD = 128
EPSILON = 1e-06
ROPE_BASE = 500000.0
NEGATIVE = -1e30
block_limit = 512


def times_plain(left, right):
    return jnp.dot(left, right, preferred_element_type=jnp.float32)


def times_transposed(left, right):
    return lax.dot_general(
        left, right, (((1,), (1,)), ((), ())), preferred_element_type=jnp.float32
    )


def transposed_times(left, right):
    return lax.dot_general(
        left, right, (((0,), (0,)), ((), ())), preferred_element_type=jnp.float32
    )


def rotation(positions):
    half_dim = HD // 2
    inverse = ROPE_BASE ** (-(jnp.arange(half_dim).astype(jnp.float32) * 2.0) / HD)
    angles = positions.astype(jnp.float32)[:, None] * inverse[None, :]
    return (jnp.cos(angles), jnp.sin(angles))


def rotate(values, cosine_table, sine_table, direction):
    row_count, local_width = values.shape
    local_heads = local_width // HD
    half_dim = HD // 2
    shaped = values.reshape(row_count, local_heads, HD)
    lower_half = shaped[..., :half_dim]
    upper_half = shaped[..., half_dim:]
    cosine_rows = cosine_table[:, None, :]
    sine_rows = direction * sine_table[:, None, :]
    rotated = jnp.concatenate(
        [
            lower_half * cosine_rows - upper_half * sine_rows,
            upper_half * cosine_rows + lower_half * sine_rows,
        ],
        axis=-1,
    )
    return rotated.reshape(row_count, local_width)


def allowed_pairs(segment_block, position_block, segments, positions):
    shared = (segments[None, :] == 0) | (segments[None, :] == segment_block[:, None])
    return shared & (positions[None, :] <= position_block[:, None])


def norm_back(incoming, values, norm_scale, gain_vector):
    scaled = gain_vector * incoming
    inner_mean = jnp.mean(scaled * values, axis=-1, keepdims=True)
    grad_values = norm_scale * scaled - values * norm_scale * norm_scale * norm_scale * inner_mean
    return (grad_values, jnp.sum(incoming * values * norm_scale, axis=0))


def spread_share(values, start):
    return lax.dynamic_update_slice_in_dim(jnp.zeros((D,), jnp.float32), values, start, 0)


def attend(query_rot, key_rot, value_low, segments, positions):
    row_count, local_width = query_rot.shape
    local_heads = local_width // HD
    block_rows = min(block_limit, row_count)
    blocks = row_count // block_rows
    key_heads = key_rot.reshape(row_count, local_heads, HD)
    value_heads = value_low.reshape(row_count, local_heads, HD)

    def one_block(packed):
        query_block, segment_block, position_block = packed
        query_heads = query_block.reshape(block_rows, local_heads, HD)
        scores = jnp.einsum(
            "qhd,khd->hqk", query_heads, key_heads, preferred_element_type=jnp.float32
        ) * HD ** (-0.5)
        allowed = allowed_pairs(segment_block, position_block, segments, positions)
        scores = jnp.where(allowed[None], scores, NEGATIVE)
        row_max = jnp.max(scores, axis=-1, keepdims=True)
        exponent = jnp.exp(scores - row_max)
        row_total = jnp.sum(exponent, axis=-1, keepdims=True)
        attn_probs = exponent / row_total
        context = jnp.einsum(
            "hqk,khd->qhd",
            attn_probs.astype(jnp.bfloat16),
            value_heads,
            preferred_element_type=jnp.float32,
        )
        return (context.reshape(block_rows, local_width), (row_max + jnp.log(row_total))[..., 0])

    context, log_norm = lax.map(
        one_block,
        (
            query_rot.reshape(blocks, block_rows, local_width),
            segments.reshape(blocks, block_rows),
            positions.reshape(blocks, block_rows),
        ),
    )
    return (context.reshape(row_count, local_width), log_norm)


def attend_back(query_rot, key_rot, value_low, context_grad, log_norm, segments, positions):
    row_count, local_width = query_rot.shape
    local_heads = local_width // HD
    block_rows = min(block_limit, row_count)
    blocks = row_count // block_rows
    scale_factor = HD ** (-0.5)
    key_heads = key_rot.reshape(row_count, local_heads, HD)
    value_heads = value_low.reshape(row_count, local_heads, HD)

    def one_block(carry, packed):
        key_total, value_total = carry
        query_block, grad_block, norm_block, segment_block, position_block = packed
        query_heads = query_block.reshape(block_rows, local_heads, HD)
        grad_heads = grad_block.reshape(block_rows, local_heads, HD)
        scores = (
            jnp.einsum("qhd,khd->hqk", query_heads, key_heads, preferred_element_type=jnp.float32)
            * scale_factor
        )
        allowed = allowed_pairs(segment_block, position_block, segments, positions)
        scores = jnp.where(allowed[None], scores, NEGATIVE)
        attn_probs = jnp.exp(scores - norm_block[..., None])
        prob_grad = jnp.einsum(
            "qhd,khd->hqk", grad_heads, value_heads, preferred_element_type=jnp.float32
        )
        delta_sum = jnp.sum(attn_probs * prob_grad, axis=-1, keepdims=True)
        score_grad = (attn_probs * (prob_grad - delta_sum)).astype(jnp.bfloat16)
        query_grad = (
            jnp.einsum("hqk,khd->qhd", score_grad, key_heads, preferred_element_type=jnp.float32)
            * scale_factor
        )
        key_total = (
            key_total
            + jnp.einsum(
                "hqk,qhd->khd", score_grad, query_heads, preferred_element_type=jnp.float32
            )
            * scale_factor
        )
        value_total = value_total + jnp.einsum(
            "hqk,qhd->khd",
            attn_probs.astype(jnp.bfloat16),
            grad_heads,
            preferred_element_type=jnp.float32,
        )
        return ((key_total, value_total), query_grad.reshape(block_rows, local_width))

    zeros_heads = jnp.zeros((row_count, local_heads, HD), jnp.float32)
    packed = (
        query_rot.reshape(blocks, block_rows, local_width),
        context_grad.reshape(blocks, block_rows, local_width),
        log_norm,
        segments.reshape(blocks, block_rows),
        positions.reshape(blocks, block_rows),
    )
    (key_grad, value_grad), query_grad = lax.scan(one_block, (zeros_heads, zeros_heads), packed)
    return (
        query_grad.reshape(row_count, local_width),
        key_grad.reshape(row_count, local_width),
        value_grad.reshape(row_count, local_width),
    )


def body(
    tokens,
    weight_query,
    weight_key,
    weight_value,
    weight_output,
    weight_gate,
    weight_up,
    weight_down,
    gain_query,
    gain_key,
    gain_attention,
    gain_feedforward,
    positions,
    segments,
    cotangent,
):
    col_width = tokens.shape[1]
    col_start = lax.axis_index("col") * col_width
    features = lax.all_gather(tokens, "col", axis=1, tiled=True)
    query_matrix, key_matrix, value_matrix, output_matrix, gate_matrix, up_matrix, down_matrix = (
        lax.all_gather(weight_query, "row", axis=0, tiled=True),
        lax.all_gather(weight_key, "row", axis=0, tiled=True),
        lax.all_gather(weight_value, "row", axis=0, tiled=True),
        lax.all_gather(weight_output, "row", axis=1, tiled=True),
        lax.all_gather(weight_gate, "row", axis=0, tiled=True),
        lax.all_gather(weight_up, "row", axis=0, tiled=True),
        lax.all_gather(weight_down, "row", axis=1, tiled=True),
    )
    query_raw = times_plain(features, query_matrix)
    key_raw = times_plain(features, key_matrix)
    value_low = times_plain(features, value_matrix).astype(jnp.bfloat16)
    square_sums = lax.psum(
        (jnp.sum(query_raw * query_raw, axis=-1), jnp.sum(key_raw * key_raw, axis=-1)), "col"
    )
    query_scale = lax.rsqrt(square_sums[0] / D + EPSILON)[:, None]
    key_scale = lax.rsqrt(square_sums[1] / D + EPSILON)[:, None]
    cosine_table, sine_table = rotation(positions)
    query_rot = rotate(query_raw * query_scale * gain_query, cosine_table, sine_table, 1.0).astype(
        jnp.bfloat16
    )
    key_rot = rotate(key_raw * key_scale * gain_key, cosine_table, sine_table, 1.0).astype(
        jnp.bfloat16
    )
    context, log_norm = attend(query_rot, key_rot, value_low, segments, positions)
    context_low = context.astype(jnp.bfloat16)
    attention_part = times_plain(context_low, output_matrix)
    attention_out = lax.psum(attention_part, "col")
    attention_scale = lax.rsqrt(
        jnp.mean(attention_out * attention_out, axis=-1, keepdims=True) + EPSILON
    )
    hidden_state = features.astype(jnp.float32) + attention_out * attention_scale * gain_attention
    hidden_low = hidden_state.astype(jnp.bfloat16)
    gate = times_plain(hidden_low, gate_matrix)
    up_rows = times_plain(hidden_low, up_matrix)
    sigmoid_gate = jax.nn.sigmoid(gate)
    silu_gate = gate * sigmoid_gate
    activated = (silu_gate * up_rows).astype(jnp.bfloat16)
    feedforward_part = times_plain(activated, down_matrix)
    feedforward_out = lax.psum(feedforward_part, "col")
    feedforward_scale = lax.rsqrt(
        jnp.mean(feedforward_out * feedforward_out, axis=-1, keepdims=True) + EPSILON
    )
    result = hidden_state + feedforward_out * feedforward_scale * gain_feedforward
    activations = lax.dynamic_slice_in_dim(result, col_start, col_width, 1).astype(jnp.bfloat16)
    upstream = lax.all_gather(cotangent, "col", axis=1, tiled=True).astype(jnp.float32)
    feedforward_full_grad, feedforward_gain_full = norm_back(
        upstream, feedforward_out, feedforward_scale, gain_feedforward
    )
    feedforward_gain_part = lax.dynamic_slice_in_dim(feedforward_gain_full, col_start, col_width, 0)
    feedforward_grad = feedforward_full_grad.astype(jnp.bfloat16)
    activated_grad = times_transposed(feedforward_grad, down_matrix)
    down_weight_grad = transposed_times(activated, feedforward_grad)
    gate_grad = (
        activated_grad * up_rows * sigmoid_gate * (1.0 + gate * (1.0 - sigmoid_gate))
    ).astype(jnp.bfloat16)
    up_grad = (activated_grad * silu_gate).astype(jnp.bfloat16)
    hidden_part = times_transposed(gate_grad, gate_matrix) + times_transposed(up_grad, up_matrix)
    gate_weight_grad = transposed_times(hidden_low, gate_grad)
    up_weight_grad = transposed_times(hidden_low, up_grad)
    hidden_grad = lax.psum(hidden_part, "col") + upstream
    attention_full_grad, attention_gain_full = norm_back(
        hidden_grad, attention_out, attention_scale, gain_attention
    )
    attention_gain_part = lax.dynamic_slice_in_dim(attention_gain_full, col_start, col_width, 0)
    attention_grad = attention_full_grad.astype(jnp.bfloat16)
    residual_grad = lax.dynamic_slice_in_dim(hidden_grad, col_start, col_width, 1)
    context_grad = times_transposed(attention_grad, output_matrix).astype(jnp.bfloat16)
    output_weight_grad = transposed_times(context_low, attention_grad)
    query_rot_grad, key_rot_grad, value_grad = attend_back(
        query_rot, key_rot, value_low, context_grad, log_norm, segments, positions
    )
    value_grad = value_grad.astype(jnp.bfloat16)
    query_norm_grad = rotate(query_rot_grad, cosine_table, sine_table, -1.0)
    key_norm_grad = rotate(key_rot_grad, cosine_table, sine_table, -1.0)
    query_scaled = gain_query * query_norm_grad
    key_scaled = gain_key * key_norm_grad
    inner_sums = lax.psum(
        (jnp.sum(query_scaled * query_raw, axis=-1), jnp.sum(key_scaled * key_raw, axis=-1)), "col"
    )
    query_raw_grad = (
        query_scale * query_scaled
        - query_raw * query_scale * query_scale * query_scale * (inner_sums[0] / D)[:, None]
    ).astype(jnp.bfloat16)
    key_raw_grad = (
        key_scale * key_scaled
        - key_raw * key_scale * key_scale * key_scale * (inner_sums[1] / D)[:, None]
    ).astype(jnp.bfloat16)
    query_gain_part = jnp.sum(query_norm_grad * query_raw * query_scale, axis=0)
    key_gain_part = jnp.sum(key_norm_grad * key_raw * key_scale, axis=0)
    input_part = (
        times_transposed(query_raw_grad, query_matrix)
        + times_transposed(key_raw_grad, key_matrix)
        + times_transposed(value_grad, value_matrix)
    )
    query_weight_part = transposed_times(features, query_raw_grad)
    key_weight_part = transposed_times(features, key_raw_grad)
    value_weight_part = transposed_times(features, value_grad)
    input_grad = (
        lax.psum_scatter(
            input_part.astype(jnp.bfloat16), "col", scatter_dimension=1, tiled=True
        ).astype(jnp.float32)
        + residual_grad
    )
    weight_grads = (
        lax.psum_scatter(
            query_weight_part.astype(jnp.bfloat16), "row", scatter_dimension=0, tiled=True
        ).astype(jnp.float32),
        lax.psum_scatter(
            key_weight_part.astype(jnp.bfloat16), "row", scatter_dimension=0, tiled=True
        ).astype(jnp.float32),
        lax.psum_scatter(
            value_weight_part.astype(jnp.bfloat16), "row", scatter_dimension=0, tiled=True
        ).astype(jnp.float32),
        lax.psum_scatter(
            output_weight_grad.astype(jnp.bfloat16), "row", scatter_dimension=1, tiled=True
        ).astype(jnp.float32),
        lax.psum_scatter(
            gate_weight_grad.astype(jnp.bfloat16), "row", scatter_dimension=0, tiled=True
        ).astype(jnp.float32),
        lax.psum_scatter(
            up_weight_grad.astype(jnp.bfloat16), "row", scatter_dimension=0, tiled=True
        ).astype(jnp.float32),
        lax.psum_scatter(
            down_weight_grad.astype(jnp.bfloat16), "row", scatter_dimension=1, tiled=True
        ).astype(jnp.float32),
    )
    gain_totals = lax.psum(
        (
            spread_share(query_gain_part, col_start),
            spread_share(key_gain_part, col_start),
            spread_share(attention_gain_part, col_start),
            spread_share(feedforward_gain_part, col_start),
        ),
        ("row", "col"),
    )
    query_gain_grad = lax.dynamic_slice_in_dim(gain_totals[0], col_start, col_width, 0)
    key_gain_grad = lax.dynamic_slice_in_dim(gain_totals[1], col_start, col_width, 0)
    return (
        activations,
        input_grad,
        weight_grads[0],
        weight_grads[1],
        weight_grads[2],
        weight_grads[3],
        weight_grads[4],
        weight_grads[5],
        weight_grads[6],
        query_gain_grad,
        key_gain_grad,
        gain_totals[2],
        gain_totals[3],
    )


def solution(mesh):
    in_specs = (
        P("row", "col"),
        P("row", "col"),
        P("row", "col"),
        P("row", "col"),
        P("col", "row"),
        P("row", "col"),
        P("row", "col"),
        P("col", "row"),
        P("col"),
        P("col"),
        P(),
        P(),
        P("row"),
        P("row"),
        P("row", "col"),
    )
    out_specs = (
        P("row", "col"),
        P("row", "col"),
        P("row", "col"),
        P("row", "col"),
        P("row", "col"),
        P("col", "row"),
        P("row", "col"),
        P("row", "col"),
        P("col", "row"),
        P("col"),
        P("col"),
        P(),
        P(),
    )
    return jax.shard_map(body, mesh=mesh, in_specs=in_specs, out_specs=out_specs, check_vma=False)
```

profile of v0, /device:TPU:0, one launch (start us, length us, event | category | flops | bytes accessed | tf_op | source)
XLA Modules:
  0.0 2133.4 jit_solution(11342082336165431979)
XLA Ops:
  17.7 23.7 %all-gather.12.cloned.1.call-done = bf16[2048,512]{1,0:T(8,128)(2,1)} async-done(((bf16[256,512]{1,0:T(8,128)(2,1)}), bf16[2048,512]{1,0:T(8,128)(2,1)}) %all-gather.12.cloned.1.call-update) | async-done | bytes 2097168 | tf_op jit(solution)/shard_map/all_gather | solution.py:193
  41.5 71.2 %all-gather.10.cloned.1.call-done = bf16[1536,2048]{1,0:T(8,128)(2,1)} async-done(((bf16[1536,512]{1,0:T(8,128)(2,1)}), bf16[1536,2048]{1,0:T(8,128)(2,1)}) %all-gather.10.cloned.1.call-update) | async-done | bytes 6291472 | tf_op jit(solution)/shard_map/all_gather | solution.py:191
  119.0 24.5 %all-gather.14.cloned.1.call-done = bf16[2048,512]{1,0:T(8,128)(2,1)} async-done(((bf16[256,512]{1,0:T(8,128)(2,1)}), bf16[2048,512]{1,0:T(8,128)(2,1)}) %all-gather.14.cloned.1.call-update) | async-done | bytes 2097168 | tf_op jit(solution)/shard_map/all_gather | solution.py:194
  211.1 47.7 %while.29 = (s32[]{:T(128)}, bf16[3,512,512]{2,1,0:T(8,128)(2,1)}, f32[3,4,512]{2,1,0:T(4,128)}, s32[1536]{0:T(1024)S(1)}, s32[3,512]{1,0:T(4,128)S(1)}, /*index...) while((s32[]{:T(128)}, bf16[3,512,512]{2,1,0:T(8,128)(2,1)}, ...), condition=%wide.region_7.8_spmd.clone, body=%wide.region_4.7_spmd.sunk.clone | while | flops 1651506688 | bytes 54626440 | solution.py:100
  271.3 234.8 %all-reduce.7.cloned.1.call-done = f32[1536,2048]{1,0:T(8,128)} async-done(((f32[1536,2048]{1,0:T(8,128)}), f32[1536,2048]{1,0:T(8,128)}) %all-reduce.7.cloned.1.call-update) | async-done | bytes 12582928 | tf_op jit(solution)/shard_map/psum | solution.py:219
  524.9 64.8 %all-gather.20.cloned.1.call-done = bf16[2048,2048]{1,0:T(8,128)(2,1)} async-done(((bf16[256,2048]{1,0:T(8,128)(2,1)}), bf16[2048,2048]{1,0:T(8,128)(2,1)}) %all-gather.20.cloned.1.call-update) | async-done | bytes 8388624 | tf_op jit(solution)/shard_map/all_gather | solution.py:197
  608.7 63.2 %all-gather.22.cloned.1.call-done = bf16[2048,2048]{1,0:T(8,128)(2,1)} async-done(((bf16[256,2048]{1,0:T(8,128)(2,1)}), bf16[2048,2048]{1,0:T(8,128)(2,1)}) %all-gather.22.cloned.1.call-update) | async-done | bytes 8388624 | tf_op jit(solution)/shard_map/all_gather | solution.py:198
  671.9 23.5 %multiply_convert_fusion.3 = (bf16[1536,2048]{1,0:T(8,128)(2,1)}, f32[1536,2048]{1,0:T(8,128)}) fusion(f32[1536,2048]{1,0:T(8,128)} %fusion.36, bf16[1536,2048]{1,0:T(8,128)(2,1)} %get-tuple-element.317, bf16[2048,2048]{1,0:T(8,128)(2,1)} %all-gather.22.cloned.1.call-done), kind=kOutput, calls=%fused_computation.51 | convolution fusion | flops 12903776256 | bytes 46137344 | tf_op jit(solution)/shard_map/dot_general | solution.py:15
  695.5 59.0 %all-gather.24.cloned.1.call-done = bf16[2048,2048]{1,0:T(8,128)(2,1)} async-done(((bf16[2048,256]{1,0:T(8,128)(2,1)}), bf16[2048,2048]{1,0:T(8,128)(2,1)}) %all-gather.24.cloned.1.call-update) | async-done | bytes 8388624 | tf_op jit(solution)/shard_map/all_gather | solution.py:199
  774.4 236.7 %all-reduce.9.cloned.1.call-done = f32[1536,2048]{1,0:T(8,128)} async-done(((f32[1536,2048]{1,0:T(8,128)}), f32[1536,2048]{1,0:T(8,128)}) %all-reduce.9.cloned.1.call-update) | async-done | bytes 12582928 | tf_op jit(solution)/shard_map/psum | solution.py:231
  1016.5 66.3 %all-gather.26.cloned.1.call-done = bf16[1536,2048]{1,0:T(8,128)(2,1)} async-done(((bf16[1536,512]{1,0:T(8,128)(2,1)}), bf16[1536,2048]{1,0:T(8,128)(2,1)}) %all-gather.26.cloned.1.call-update) | async-done | bytes 6291472 | tf_op jit(solution)/shard_map/all_gather | solution.py:237
  1102.5 26.6 %multiply_convert_fusion.1 = (bf16[1536,2048]{1,0:T(8,128)(2,1)}, bf16[1536,2048]{1,0:T(8,128)(2,1)}) fusion(f32[1536,2048]{1,0:T(8,128)} %fusion.36, f32[1536,2048]{1,0:T(8,128)} %get-tuple-element.355, bf16[1536,2048]{1,0:T(8,128)(2,1)} %get-tuple-element.329, bf16[2048,2048]{1,0:T(8,128)(2,1)} %all-gather.24.cloned.1.call-done), kind=kOutput, calls=%fused_computation.48 | convolution fusion | flops 12925796352 | bytes 52428800 | tf_op jit(solution)/shard_map/dot_general | solution.py:19
  1148.4 20.7 convolution_add_fusion
  1173.6 234.9 %all-reduce.11.cloned.1.call-done = f32[1536,2048]{1,0:T(8,128)} async-done(((f32[1536,2048]{1,0:T(8,128)}), f32[1536,2048]{1,0:T(8,128)}) %all-reduce.11.cloned.1.call-update) | async-done | bytes 12582928 | tf_op jit(solution)/shard_map/psum | solution.py:252
  1436.2 127.1 %while.30 = (s32[]{:T(128)}, f32[1536,4,128]{0,2,1:T(8,128)}, f32[1536,4,128]{0,2,1:T(8,128)}, f32[3,512,512]{2,1,0:T(8,128)}, bf16[3,512,512]{1,2,0:T(8,128)(2,...) while((s32[]{:T(128)}, f32[1536,4,128]{0,2,1:T(8,128)}, ...), condition=%wide.region_17.18_spmd.clone.clone, body=%wide.region_15.17_spmd.clone.sunk.clone | while | flops 4062182912 | bytes 245442384 | solution.py:164
  1631.1 19.6 convolution_convert_fusion
  1670.6 20.3 convolution_convert_fusion.2
  1691.0 20.0 convolution_convert_fusion.1
  1758.0 41.1 %all-reduce = (f32[2048]{0:T(1024)S(1)}, f32[2048]{0:T(1024)S(1)}, f32[2048]{0:T(1024)}, f32[2048]{0:T(1024)}) all-reduce(f32[2048]{0:T(1024)S(1)} %dynamic_update_slice.23, f32[2048]{0:T(1024)S(1)} %dynamic_update_slice.24, f32[2048]{0:T(1024)S(1)} %dynamic-slice_dynamic-update-slice_fusion.1, ...), channel_id=1, replica_groups=mesh['row'=8,'col'=4] {'row','col'}, use_global_device_ids=true, to_apply=%region_31.32 | all-reduce | flops 8192 | bytes 65536 | tf_op jit(solution)/shard_map/psum | solution.py:319
  1806.8 25.9 %reduce-scatter.11.cloned.1.call-done = bf16[256,512]{0,1:T(8,128)(2,1)} async-done(((bf16[2048,512]{0,1:T(8,128)(2,1)}), bf16[256,512]{0,1:T(8,128)(2,1)}) %reduce-scatter.11.cloned.1.call-update) | async-done | bytes 262160 | tf_op jit(solution)/shard_map/reduce_scatter | solution.py:297
  1834.5 88.3 %reduce-scatter.19.cloned.1.call-done = bf16[256,2048]{1,0:T(8,128)(2,1)} async-done(((bf16[2048,2048]{1,0:T(8,128)(2,1)}), bf16[256,2048]{1,0:T(8,128)(2,1)}) %reduce-scatter.19.cloned.1.call-update) | async-done | bytes 1048592 | tf_op jit(solution)/shard_map/reduce_scatter | solution.py:309
  1925.6 87.4 %reduce-scatter.21.cloned.1.call-done = bf16[256,2048]{1,0:T(8,128)(2,1)} async-done(((bf16[2048,2048]{1,0:T(8,128)(2,1)}), bf16[256,2048]{1,0:T(8,128)(2,1)}) %reduce-scatter.21.cloned.1.call-update) | async-done | bytes 1048592 | tf_op jit(solution)/shard_map/reduce_scatter | solution.py:312
  2015.8 34.6 %reduce-scatter.15.cloned.1.call-done = bf16[256,512]{0,1:T(8,128)(2,1)} async-done(((bf16[2048,512]{0,1:T(8,128)(2,1)}), bf16[256,512]{0,1:T(8,128)(2,1)}) %reduce-scatter.15.cloned.1.call-update) | async-done | bytes 262160 | tf_op jit(solution)/shard_map/reduce_scatter | solution.py:303
  2052.3 69.5 %reduce-scatter.9.cloned.1.call-done = bf16[1536,512]{1,0:T(8,128)(2,1)} async-done(((bf16[1536,2048]{1,0:T(8,128)(2,1)}), bf16[1536,512]{1,0:T(8,128)(2,1)}) %reduce-scatter.9.cloned.1.call-update) | async-done | bytes 1572880 | tf_op jit(solution)/shard_map/reduce_scatter | solution.py:291
  (341 shorter events, 560.8 us)
Async XLA Ops:
  7.2 34.3 %all-gather.12.cloned.1.call-start = ((), (), s32[]{:S(2)}) async-start(), calls=%async_computation.9 | async-start | bytes 2359296 | tf_op jit(solution)/shard_map/all_gather | solution.py:193
  7.9 104.7 %all-gather.10.cloned.1.call-start = ((), (), s32[]{:S(2)}) async-start(), calls=%async_computation.8 | async-start | bytes 7864320 | tf_op jit(solution)/shard_map/all_gather | solution.py:191
  8.7 134.8 %all-gather.14.cloned.1.call-start = ((), (), s32[]{:S(2)}) async-start(), calls=%async_computation.10 | async-start | bytes 2359296 | tf_op jit(solution)/shard_map/all_gather | solution.py:194
  9.4 193.6 %all-gather.16.cloned.1.call-start = ((), (), s32[]{:S(2)}) async-start(), calls=%async_computation.11 | async-start | bytes 2359296 | tf_op jit(solution)/shard_map/all_gather | solution.py:195
  10.0 248.9 %all-gather.18.cloned.1.call-start = ((), (), s32[]{:S(2)}) async-start(), calls=%async_computation.12 | async-start | bytes 2359296 | tf_op jit(solution)/shard_map/all_gather | solution.py:196
  10.6 495.5 %all-reduce.7.cloned.1.call-start = ((), (), s32[]{:S(2)}) async-start(), calls=%async_computation.13 | async-start | bytes 25165824 | tf_op jit(solution)/shard_map/psum | solution.py:219
  269.0 320.8 %all-gather.20.cloned.1.call-start = ((), (), s32[]{:S(2)}) async-start(), calls=%async_computation.14 | async-start | bytes 9437184 | tf_op jit(solution)/shard_map/all_gather | solution.py:197
  269.7 402.2 %all-gather.22.cloned.1.call-start = ((), (), s32[]{:S(2)}) async-start(), calls=%async_computation.15 | async-start | bytes 9437184 | tf_op jit(solution)/shard_map/all_gather | solution.py:198
  270.5 484.0 %all-gather.24.cloned.1.call-start = ((), (), s32[]{:S(2)}) async-start(), calls=%async_computation.16 | async-start | bytes 9437184 | tf_op jit(solution)/shard_map/all_gather | solution.py:199
  271.2 241.1 %copy-start.42 = (f32[2048]{0:T(1024)S(1)}, f32[2048]{0:T(1024)}, u32[]{:S(2)}) copy-start(f32[2048]{0:T(1024)} %param.29) | copy-start | bytes 24580
  271.2 739.8 %all-reduce.9.cloned.1.call-start = ((), (), s32[]{:S(2)}) async-start(), calls=%async_computation.17 | async-start | bytes 25165824 | tf_op jit(solution)/shard_map/psum | solution.py:231
  773.4 309.4 %all-gather.26.cloned.1.call-start = ((), (), s32[]{:S(2)}) async-start(), calls=%async_computation.18 | async-start | bytes 7864320 | tf_op jit(solution)/shard_map/all_gather | solution.py:237
  774.2 308.6 %copy-start.44 = (f32[2048]{0:T(1024)S(1)}, f32[2048]{0:T(1024)}, u32[]{:S(2)}) copy-start(f32[2048]{0:T(1024)} %param.30) | copy-start | bytes 24580
  774.2 634.3 %all-reduce.11.cloned.1.call-start = ((), (), s32[]{:S(2)}) async-start(), calls=%async_computation.19 | async-start | bytes 25165824 | tf_op jit(solution)/shard_map/psum | solution.py:252
  1169.1 631.3 %reduce-scatter.13.cloned.1.call-start = ((), (), s32[]{:S(2)}) async-start(), calls=%async_computation.22 | async-start | bytes 2359296 | tf_op jit(solution)/shard_map/reduce_scatter | solution.py:300
  1170.5 238.1 %copy-start.39 = (f32[1536]{0:T(1024)S(1)}, f32[1536]{0:T(1024)}, u32[]{:S(2)}) copy-start(f32[1536]{0:T(1024)} %copy-done.38) | copy-start | bytes 18436
  1170.5 238.1 %copy-start.43 = (f32[2048]{0:T(1024)S(1)}, f32[2048]{0:T(1024)}, u32[]{:S(2)}) copy-start(f32[2048]{0:T(1024)} %param.29) | copy-start | bytes 24580
  1631.1 171.2 %reduce-scatter.23.cloned.1.call-start = ((), (), s32[]{:S(2)}) async-start(), calls=%async_computation.27 | async-start | bytes 9437184 | tf_op jit(solution)/shard_map/reduce_scatter | solution.py:315
  1650.8 154.2 %reduce-scatter.17.cloned.1.call-start = ((), (), s32[]{:S(2)}) async-start(), calls=%async_computation.24 | async-start | bytes 2359296 | tf_op jit(solution)/shard_map/reduce_scatter | solution.py:306
  1659.0 173.6 %reduce-scatter.11.cloned.1.call-start = ((), (), s32[]{:S(2)}) async-start(), calls=%async_computation.21 | async-start | bytes 2359296 | tf_op jit(solution)/shard_map/reduce_scatter | solution.py:297
  1670.6 252.3 %reduce-scatter.19.cloned.1.call-start = ((), (), s32[]{:S(2)}) async-start(), calls=%async_computation.25 | async-start | bytes 9437184 | tf_op jit(solution)/shard_map/reduce_scatter | solution.py:309
  1691.0 322.0 %reduce-scatter.21.cloned.1.call-start = ((), (), s32[]{:S(2)}) async-start(), calls=%async_computation.26 | async-start | bytes 9437184 | tf_op jit(solution)/shard_map/reduce_scatter | solution.py:312
  1711.0 339.4 %reduce-scatter.15.cloned.1.call-start = ((), (), s32[]{:S(2)}) async-start(), calls=%async_computation.23 | async-start | bytes 2359296 | tf_op jit(solution)/shard_map/reduce_scatter | solution.py:303
  1721.8 400.0 %reduce-scatter.9.cloned.1.call-start = ((), (), s32[]{:S(2)}) async-start(), calls=%async_computation.20 | async-start | bytes 7864320 | tf_op jit(solution)/shard_map/reduce_scatter | solution.py:291
  (62 other events, 442.5 us)
Sparse Core Ops, SparseCore 0:
  9.6 31.8 all-gather.11
  43.3 69.3 all-gather.9
  114.3 29.1 all-gather.13
  144.9 28.5 all-gather.15
  174.9 30.0 all-gather.17
  269.1 236.9 all-reduce.6
  507.7 82.0 all-gather.19
  591.4 80.5 all-gather.21
  673.5 80.9 all-gather.23
  773.6 237.4 all-reduce.8
  1012.9 69.8 all-gather.25
  1169.2 239.2 all-reduce.10
  1631.2 36.1 reduce-scatter.12
  1669.5 87.8 reduce-scatter.22
  1760.1 34.8 reduce-scatter.16
  1797.7 34.8 reduce-scatter.10
  1834.8 88.0 reduce-scatter.18
  1925.0 87.9 reduce-scatter.20
  2015.9 34.5 reduce-scatter.14
  2053.3 68.5 reduce-scatter.8
where the time goes:
time: 2140 us; the launch traced here: 2130 us
  waiting for transfers between devices  1390 us (65%)
  matrix products  384 us (18%)
  other arithmetic  160 us (7%)
  local copies, waits for them, and re-layouts  109 us (5%)
  blocking collectives  72.4 us (3%)
    psum x1, waiting for transfers between devices, body(): feedforward_out = lax.psum(feedforward_part, 'col')  237 us
    psum x1, waiting for transfers between devices, body(): hidden_grad = lax.psum(hidden_part, 'col') + upstream  235 us
    psum x1, waiting for transfers between devices, body(): attention_out = lax.psum(attention_part, 'col')  235 us
    dot_general x7, matrix products, times_transposed(): lax.dot_general(left, right, (((1,), (1,)), ((), ())), preferred_element_...  99.4 us
    dot_general x7, matrix products, times_plain(): return jnp.dot(left, right, preferred_element_type=jnp.float32)  94.4 us
    dot_general x7, matrix products, transposed_times(): lax.dot_general(left, right, (((0,), (0,)), ((), ())), preferred_element_...  90.8 us
    reduce_scatter x1, waiting for transfers between devices, body(): lax.psum_scatter(gate_weight_grad.astype(jnp.bfloat16), 'row', scatter_di...  88.3 us
    reduce_scatter x1, waiting for transfers between devices, body(): lax.psum_scatter(up_weight_grad.astype(jnp.bfloat16), 'row', scatter_dime...  87.4 us
  transfers between devices with their start and end apart: 20, of which 15 were waited for; matrix products, arithmetic and copies ran while one was open for 15% of the time, Pallas kernels for 0%

commit v1 on v0

--- a/solution.py
+++ b/solution.py
@@ -216,7 +216,7 @@
     context, log_norm = attend(query_rot, key_rot, value_low, segments, positions)
     context_low = context.astype(jnp.bfloat16)
     attention_part = times_plain(context_low, output_matrix)
-    attention_out = lax.psum(attention_part, "col")
+    attention_out = jnp.sum(lax.all_gather(attention_part, "col"), axis=0)
     attention_scale = lax.rsqrt(
         jnp.mean(attention_out * attention_out, axis=-1, keepdims=True) + EPSILON
     )

time: 2140 us -> 2250 us (1.051)
  waiting for transfers between devices: 1390 us -> 1480 us
  other arithmetic: 160 us -> 186 us
    all_gather x0 -> x1, waiting for transfers between devices: none -> 432 us  [body(): attention_out = jnp.sum(lax.all_gather(attention_part, 'col'), axis=0)]
    psum x1 -> x0, waiting for transfers between devices: 235 us -> none  [body(): attention_out = lax.psum(attention_part, 'col')]
    reduce_scatter x1, waiting for transfers between devices: 88.3 us -> 10.7 us  [body(): lax.psum_scatter(gate_weight_grad.astype(jnp.bfloat16), 'row', scatter_di...]
    reduce_sum x0 -> x1, other arithmetic: none -> 24.1 us  [body(): attention_out = jnp.sum(lax.all_gather(attention_part, 'col'), axis=0)]
    all_gather x1, waiting for transfers between devices: 64.8 us -> 41.2 us  [body(): lax.all_gather(weight_gate, 'row', axis=0, tiled=True)]
  transfers between devices with their start and end apart: 20 -> 20, of which waited for: 15 -> 15; matrix products, arithmetic and copies ran while one was open for 15% -> 24% of each run, Pallas kernels for 0% -> 0%
where the time goes in v1:
time: 2250 us; the launch traced here: 2240 us
  waiting for transfers between devices  1480 us (66%)
  matrix products  384 us (17%)
  other arithmetic  186 us (8%)
  local copies, waits for them, and re-layouts  107 us (5%)
  blocking collectives  73.2 us (3%)
    all_gather x1, waiting for transfers between devices, body(): attention_out = jnp.sum(lax.all_gather(attention_part, 'col'), axis=0)  432 us
    psum x1, waiting for transfers between devices, body(): feedforward_out = lax.psum(feedforward_part, 'col')  237 us
    psum x1, waiting for transfers between devices, body(): hidden_grad = lax.psum(hidden_part, 'col') + upstream  214 us
    dot_general x7, matrix products, times_transposed(): lax.dot_general(left, right, (((1,), (1,)), ((), ())), preferred_element_...  98.9 us
    dot_general x7, matrix products, times_plain(): return jnp.dot(left, right, preferred_element_type=jnp.float32)  94.7 us
    dot_general x7, matrix products, transposed_times(): lax.dot_general(left, right, (((0,), (0,)), ((), ())), preferred_element_...  90.8 us
    reduce_scatter x1, waiting for transfers between devices, body(): lax.psum_scatter(up_weight_grad.astype(jnp.bfloat16), 'row', scatter_dime...  87.4 us
    all_gather x1, waiting for transfers between devices, body(): features = lax.all_gather(tokens, 'col', axis=1, tiled=True)  71.2 us
  transfers between devices with their start and end apart: 20, of which 15 were waited for; matrix products, arithmetic and copies ran while one was open for 24% of the time, Pallas kernels for 0%

profile of v1, /device:TPU:0, one launch (start us, length us, event | category | flops | bytes accessed | tf_op | source)
XLA Modules:
  0.0 2242.8 jit_solution(16239942140528250872)
XLA Ops:
  17.7 23.8 %all-gather.14.cloned.1.call-done = bf16[2048,512]{1,0:T(8,128)(2,1)} async-done(((bf16[256,512]{1,0:T(8,128)(2,1)}), bf16[2048,512]{1,0:T(8,128)(2,1)}) %all-gather.14.cloned.1.call-update) | async-done | bytes 2097168 | tf_op jit(solution)/shard_map/all_gather | solution.py:193
  41.5 71.2 %all-gather.12.cloned.1.call-done = bf16[1536,2048]{1,0:T(8,128)(2,1)} async-done(((bf16[1536,512]{1,0:T(8,128)(2,1)}), bf16[1536,2048]{1,0:T(8,128)(2,1)}) %all-gather.12.cloned.1.call-update) | async-done | bytes 6291472 | tf_op jit(solution)/shard_map/all_gather | solution.py:191
  119.0 24.5 %all-gather.16.cloned.1.call-done = bf16[2048,512]{1,0:T(8,128)(2,1)} async-done(((bf16[256,512]{1,0:T(8,128)(2,1)}), bf16[2048,512]{1,0:T(8,128)(2,1)}) %all-gather.16.cloned.1.call-update) | async-done | bytes 2097168 | tf_op jit(solution)/shard_map/all_gather | solution.py:194
  211.2 48.1 %while.29 = (s32[]{:T(128)}, bf16[3,512,512]{2,1,0:T(8,128)(2,1)}, f32[3,4,512]{2,1,0:T(4,128)}, s32[1536]{0:T(1024)S(1)}, s32[3,512]{1,0:T(4,128)S(1)}, /*index...) while((s32[]{:T(128)}, bf16[3,512,512]{2,1,0:T(8,128)(2,1)}, ...), condition=%wide.region_7.8_spmd.clone, body=%wide.region_4.7_spmd.sunk.clone | while | flops 1651506688 | bytes 54626440 | solution.py:100
  271.6 432.4 %all-gather.30.cloned.1.call-done = f32[6144,2048]{1,0:T(8,128)} async-done(((f32[1536,2048]{1,0:T(8,128)}), f32[6144,2048]{1,0:T(8,128)}) %all-gather.30.cloned.1.call-update) | async-done | bytes 50331664 | tf_op jit(solution)/shard_map/all_gather | solution.py:219
  704.1 24.1 %reduce_sum.137 = f32[1536,2048]{1,0:T(8,128)} reduce(f32[4,1536,2048]{2,1,0:T(8,128)} %bitcast.194, f32[]{:T(128)} %constant.46.clone.1), dimensions={0}, to_apply=%region_8.9 | reduce | flops 9437184 | bytes 62914564 | tf_op jit(solution)/shard_map/reduce_sum | solution.py:219
  746.5 41.2 %all-gather.22.cloned.1.call-done = bf16[2048,2048]{1,0:T(8,128)(2,1)} async-done(((bf16[256,2048]{1,0:T(8,128)(2,1)}), bf16[2048,2048]{1,0:T(8,128)(2,1)}) %all-gather.22.cloned.1.call-update) | async-done | bytes 8388624 | tf_op jit(solution)/shard_map/all_gather | solution.py:197
  806.8 63.0 %all-gather.24.cloned.1.call-done = bf16[2048,2048]{1,0:T(8,128)(2,1)} async-done(((bf16[256,2048]{1,0:T(8,128)(2,1)}), bf16[2048,2048]{1,0:T(8,128)(2,1)}) %all-gather.24.cloned.1.call-update) | async-done | bytes 8388624 | tf_op jit(solution)/shard_map/all_gather | solution.py:198
  869.9 23.6 %multiply_convert_fusion.3 = (bf16[1536,2048]{1,0:T(8,128)(2,1)}, f32[1536,2048]{1,0:T(8,128)}) fusion(f32[1536,2048]{1,0:T(8,128)} %fusion.36, bf16[1536,2048]{1,0:T(8,128)(2,1)} %get-tuple-element.317, bf16[2048,2048]{1,0:T(8,128)(2,1)} %all-gather.24.cloned.1.call-done), kind=kOutput, calls=%fused_computation.51 | convolution fusion | flops 12903776256 | bytes 46137344 | tf_op jit(solution)/shard_map/dot_general | solution.py:15
  893.4 59.0 %all-gather.26.cloned.1.call-done = bf16[2048,2048]{1,0:T(8,128)(2,1)} async-done(((bf16[2048,256]{1,0:T(8,128)(2,1)}), bf16[2048,2048]{1,0:T(8,128)(2,1)}) %all-gather.26.cloned.1.call-update) | async-done | bytes 8388624 | tf_op jit(solution)/shard_map/all_gather | solution.py:199
  972.4 236.8 %all-reduce.6.cloned.1.call-done = f32[1536,2048]{1,0:T(8,128)} async-done(((f32[1536,2048]{1,0:T(8,128)}), f32[1536,2048]{1,0:T(8,128)}) %all-reduce.6.cloned.1.call-update) | async-done | bytes 12582928 | tf_op jit(solution)/shard_map/psum | solution.py:231
  1214.7 66.3 %all-gather.28.cloned.1.call-done = bf16[1536,2048]{1,0:T(8,128)(2,1)} async-done(((bf16[1536,512]{1,0:T(8,128)(2,1)}), bf16[1536,2048]{1,0:T(8,128)(2,1)}) %all-gather.28.cloned.1.call-update) | async-done | bytes 6291472 | tf_op jit(solution)/shard_map/all_gather | solution.py:237
  1300.8 26.4 %multiply_convert_fusion.1 = (bf16[1536,2048]{1,0:T(8,128)(2,1)}, bf16[1536,2048]{1,0:T(8,128)(2,1)}) fusion(f32[1536,2048]{1,0:T(8,128)} %fusion.36, f32[1536,2048]{1,0:T(8,128)} %get-tuple-element.355, bf16[1536,2048]{1,0:T(8,128)(2,1)} %get-tuple-element.329, bf16[2048,2048]{1,0:T(8,128)(2,1)} %all-gather.26.cloned.1.call-done), kind=kOutput, calls=%fused_computation.48 | convolution fusion | flops 12925796352 | bytes 52428800 | tf_op jit(solution)/shard_map/dot_general | solution.py:19
  1346.4 20.5 convolution_add_fusion
  1371.4 20.4 convolution_convert_fusion
  1391.9 214.5 %all-reduce.8.cloned.1.call-done = f32[1536,2048]{1,0:T(8,128)} async-done(((f32[1536,2048]{1,0:T(8,128)}), f32[1536,2048]{1,0:T(8,128)}) %all-reduce.8.cloned.1.call-update) | async-done | bytes 12582928 | tf_op jit(solution)/shard_map/psum | solution.py:252
  1635.1 127.7 %while.30 = (s32[]{:T(128)}, f32[1536,4,128]{0,2,1:T(8,128)}, f32[1536,4,128]{0,2,1:T(8,128)}, f32[3,512,512]{2,1,0:T(8,128)}, bf16[3,512,512]{1,2,0:T(8,128)(2,...) while((s32[]{:T(128)}, f32[1536,4,128]{0,2,1:T(8,128)}, ...), condition=%wide.region_17.18_spmd.clone.clone, body=%wide.region_15.17_spmd.clone.sunk.clone | while | flops 4062182912 | bytes 245442384 | solution.py:164
  1838.8 19.6 convolution_convert_fusion.2
  1858.4 19.9 convolution_convert_fusion.1
  1935.1 41.8 %all-reduce = (f32[2048]{0:T(1024)S(1)}, f32[2048]{0:T(1024)S(1)}, f32[2048]{0:T(1024)}, f32[2048]{0:T(1024)}) all-reduce(f32[2048]{0:T(1024)S(1)} %dynamic_update_slice.23, f32[2048]{0:T(1024)S(1)} %dynamic_update_slice.24, f32[2048]{0:T(1024)S(1)} %dynamic-slice_dynamic-update-slice_fusion.1, ...), channel_id=1, replica_groups=mesh['row'=8,'col'=4] {'row','col'}, use_global_device_ids=true, to_apply=%region_31.32 | all-reduce | flops 8192 | bytes 65536 | tf_op jit(solution)/shard_map/psum | solution.py:319
  1998.1 87.4 %reduce-scatter.21.cloned.1.call-done = bf16[256,2048]{1,0:T(8,128)(2,1)} async-done(((bf16[2048,2048]{1,0:T(8,128)(2,1)}), bf16[256,2048]{1,0:T(8,128)(2,1)}) %reduce-scatter.21.cloned.1.call-update) | async-done | bytes 1048592 | tf_op jit(solution)/shard_map/reduce_scatter | solution.py:312
  2088.3 34.4 %reduce-scatter.11.cloned.1.call-done = bf16[256,512]{0,1:T(8,128)(2,1)} async-done(((bf16[2048,512]{0,1:T(8,128)(2,1)}), bf16[256,512]{0,1:T(8,128)(2,1)}) %reduce-scatter.11.cloned.1.call-update) | async-done | bytes 262160 | tf_op jit(solution)/shard_map/reduce_scatter | solution.py:297
  2124.5 35.2 %reduce-scatter.15.cloned.1.call-done = bf16[256,512]{0,1:T(8,128)(2,1)} async-done(((bf16[2048,512]{0,1:T(8,128)(2,1)}), bf16[256,512]{0,1:T(8,128)(2,1)}) %reduce-scatter.15.cloned.1.call-update) | async-done | bytes 262160 | tf_op jit(solution)/shard_map/reduce_scatter | solution.py:303
  2161.6 69.7 %reduce-scatter.9.cloned.1.call-done = bf16[1536,512]{1,0:T(8,128)(2,1)} async-done(((bf16[1536,2048]{1,0:T(8,128)(2,1)}), bf16[1536,512]{1,0:T(8,128)(2,1)}) %reduce-scatter.9.cloned.1.call-update) | async-done | bytes 1572880 | tf_op jit(solution)/shard_map/reduce_scatter | solution.py:291
  (340 shorter events, 571.1 us)
Async XLA Ops:
  7.2 34.3 %all-gather.14.cloned.1.call-start = ((), (), s32[]{:S(2)}) async-start(), calls=%async_computation.9 | async-start | bytes 2359296 | tf_op jit(solution)/shard_map/all_gather | solution.py:193
  7.9 104.7 %all-gather.12.cloned.1.call-start = ((), (), s32[]{:S(2)}) async-start(), calls=%async_computation.8 | async-start | bytes 7864320 | tf_op jit(solution)/shard_map/all_gather | solution.py:191
  8.7 134.8 %all-gather.16.cloned.1.call-start = ((), (), s32[]{:S(2)}) async-start(), calls=%async_computation.10 | async-start | bytes 2359296 | tf_op jit(solution)/shard_map/all_gather | solution.py:194
  9.4 193.7 %all-gather.18.cloned.1.call-start = ((), (), s32[]{:S(2)}) async-start(), calls=%async_computation.11 | async-start | bytes 2359296 | tf_op jit(solution)/shard_map/all_gather | solution.py:195
  10.0 249.3 %all-gather.20.cloned.1.call-start = ((), (), s32[]{:S(2)}) async-start(), calls=%async_computation.12 | async-start | bytes 2359296 | tf_op jit(solution)/shard_map/all_gather | solution.py:196
  10.6 693.5 %all-gather.30.cloned.1.call-start = ((), (), s32[]{:S(2)}) async-start(), calls=%async_computation.27 | async-start | bytes 62914560 | tf_op jit(solution)/shard_map/all_gather | solution.py:219
  118.9 49.5 %copy-start.11 = (f32[1536,512]{0,1:T(8,128)}, f32[1536,512]{0,1:T(8,128)S(1)}, u32[]{:S(2)}) copy-start(f32[1536,512]{0,1:T(8,128)S(1)} %get-tuple-element.351) | copy-start | bytes 9437188
  269.3 518.4 %all-gather.22.cloned.1.call-start = ((), (), s32[]{:S(2)}) async-start(), calls=%async_computation.13 | async-start | bytes 9437184 | tf_op jit(solution)/shard_map/all_gather | solution.py:197
  270.1 599.8 %all-gather.24.cloned.1.call-start = ((), (), s32[]{:S(2)}) async-start(), calls=%async_computation.14 | async-start | bytes 9437184 | tf_op jit(solution)/shard_map/all_gather | solution.py:198
  270.8 681.6 %all-gather.26.cloned.1.call-start = ((), (), s32[]{:S(2)}) async-start(), calls=%async_computation.15 | async-start | bytes 9437184 | tf_op jit(solution)/shard_map/all_gather | solution.py:199
  271.6 937.7 %all-reduce.6.cloned.1.call-start = ((), (), s32[]{:S(2)}) async-start(), calls=%async_computation.16 | async-start | bytes 25165824 | tf_op jit(solution)/shard_map/psum | solution.py:231
  971.6 309.4 %all-gather.28.cloned.1.call-start = ((), (), s32[]{:S(2)}) async-start(), calls=%async_computation.17 | async-start | bytes 7864320 | tf_op jit(solution)/shard_map/all_gather | solution.py:237
  972.4 308.7 %copy-start.43 = (f32[2048]{0:T(1024)S(1)}, f32[2048]{0:T(1024)}, u32[]{:S(2)}) copy-start(f32[2048]{0:T(1024)} %param.30) | copy-start | bytes 24580
  972.4 634.0 %all-reduce.8.cloned.1.call-start = ((), (), s32[]{:S(2)}) async-start(), calls=%async_computation.18 | async-start | bytes 25165824 | tf_op jit(solution)/shard_map/psum | solution.py:252
  1366.9 611.3 %reduce-scatter.23.cloned.1.call-start = ((), (), s32[]{:S(2)}) async-start(), calls=%async_computation.26 | async-start | bytes 9437184 | tf_op jit(solution)/shard_map/reduce_scatter | solution.py:315
  1391.8 214.6 %copy-start.38 = (f32[1536]{0:T(1024)S(1)}, f32[1536]{0:T(1024)}, u32[]{:S(2)}) copy-start(f32[1536]{0:T(1024)} %copy-done.37) | copy-start | bytes 18436
  1391.8 214.6 %copy-start.42 = (f32[2048]{0:T(1024)S(1)}, f32[2048]{0:T(1024)}, u32[]{:S(2)}) copy-start(f32[2048]{0:T(1024)} %param.29) | copy-start | bytes 24580
  1391.9 589.1 %reduce-scatter.13.cloned.1.call-start = ((), (), s32[]{:S(2)}) async-start(), calls=%async_computation.21 | async-start | bytes 2359296 | tf_op jit(solution)/shard_map/reduce_scatter | solution.py:300
  1830.6 152.2 %reduce-scatter.17.cloned.1.call-start = ((), (), s32[]{:S(2)}) async-start(), calls=%async_computation.23 | async-start | bytes 2359296 | tf_op jit(solution)/shard_map/reduce_scatter | solution.py:306
  1838.7 156.6 %reduce-scatter.19.cloned.1.call-start = ((), (), s32[]{:S(2)}) async-start(), calls=%async_computation.24 | async-start | bytes 9437184 | tf_op jit(solution)/shard_map/reduce_scatter | solution.py:309
  1858.4 227.1 %reduce-scatter.21.cloned.1.call-start = ((), (), s32[]{:S(2)}) async-start(), calls=%async_computation.25 | async-start | bytes 9437184 | tf_op jit(solution)/shard_map/reduce_scatter | solution.py:312
  1878.3 244.3 %reduce-scatter.11.cloned.1.call-start = ((), (), s32[]{:S(2)}) async-start(), calls=%async_computation.20 | async-start | bytes 2359296 | tf_op jit(solution)/shard_map/reduce_scatter | solution.py:297
  1890.1 269.7 %reduce-scatter.15.cloned.1.call-start = ((), (), s32[]{:S(2)}) async-start(), calls=%async_computation.22 | async-start | bytes 2359296 | tf_op jit(solution)/shard_map/reduce_scatter | solution.py:303
  1899.0 332.3 %reduce-scatter.9.cloned.1.call-start = ((), (), s32[]{:S(2)}) async-start(), calls=%async_computation.19 | async-start | bytes 7864320 | tf_op jit(solution)/shard_map/reduce_scatter | solution.py:291
  (61 other events, 404.6 us)
Sparse Core Ops, SparseCore 0:
  9.6 31.8 all-gather.13
  43.3 69.2 all-gather.11
  114.3 29.1 all-gather.15
  144.9 28.5 all-gather.17
  174.9 29.9 all-gather.19
  269.5 434.5 all-gather.29
  705.7 82.0 all-gather.21
  789.3 80.5 all-gather.23
  871.5 80.9 all-gather.25
  971.7 237.4 all-reduce.5
  1211.1 69.8 all-gather.27
  1367.0 239.2 all-reduce.7
  1608.7 89.5 reduce-scatter.22
  1830.7 35.9 reduce-scatter.12
  1869.4 34.6 reduce-scatter.16
  1906.2 89.0 reduce-scatter.18
  1997.4 88.0 reduce-scatter.20
  2088.2 34.3 reduce-scatter.10
  2124.9 34.7 reduce-scatter.14
  2162.6 68.6 reduce-scatter.8
